TPU v7x, 32 devices: a whole 2x2x4 slice. The times are simulated.
32 devices in a mesh: dp: 4 (over y, x), tensor: 8 (over z, core).
Axes of the slice: x: 2, y: 2, z: 4, core: 2. Of those that a mesh axis runs over, the one named last changes fastest.
Arguments:
- saved_input: bfloat16 [512, 8192], P(('dp', 'tensor')), may hold values from -8 to 8
- keep_bits: int32 [512, 448], P(('dp', 'tensor')), may hold values from -2147483648 to 2147483646, as said below
- norm_gain: bfloat16 [8192], P('dp'), may hold values from 0.099609375 to 1.8984375
- gate_weight: bfloat16 [8192, 14336], P('dp', 'tensor'), may hold values from -0.0625 to 0.0625
- up_weight: bfloat16 [8192, 14336], P('dp', 'tensor'), may hold values from -0.0625 to 0.0625
- down_weight: bfloat16 [14336, 8192], P('tensor', 'dp'), may hold values from -0.046875 to 0.046875
Outputs:
- layer_out: bfloat16 [512, 8192], P('tensor', 'dp')
- row_check: float32 [512], P('tensor')
Inputs may be any that keep to these rules, and one draw needn't show every extreme that they name: `keep_bits`: bit k of word w of a token is the keep bit of hidden unit 32 w + k.
All inputs are finite; a program needn't handle non-finite values.
Results may differ from a plain program's by a relative error of at most 0.017.
Values may be sent and summed in bfloat16 or wider, within the bound.
A program may use at most 64 MiB of HBM per device.

v0:
```python
import jax
import jax.numpy as jnp
from jax import lax
from jax.sharding import PartitionSpec as P

D = 8192


def on_device(saved_input, keep_bits, norm_gain, gate_weight, up_weight, down_weight):
    tensor_width = lax.axis_size("tensor")
    dp_width = lax.axis_size("dp")
    unit_words = lax.all_to_all(keep_bits, "tensor", split_axis=1, concat_axis=0, tiled=True)
    shifts = jnp.arange(32, dtype=jnp.int32)
    keep_mask = jnp.bitwise_and(jnp.right_shift(unit_words[:, :, None], shifts[None, None, :]), 1)
    keep_mask = keep_mask.reshape(unit_words.shape[0], -1)
    keep_scale = 2.0 * keep_mask.astype(jnp.float32)
    width_units = gate_weight.shape[1]
    columns = lax.all_to_all(saved_input, "dp", split_axis=1, concat_axis=0, tiled=True)
    collected = lax.all_gather(columns, "tensor", axis=0, tiled=True)
    per_device = saved_input.shape[0]
    collected = collected.reshape(tensor_width, dp_width, per_device, collected.shape[1])
    collected = collected.transpose(1, 0, 2, 3).reshape(-1, collected.shape[3])
    widened = collected.astype(jnp.float32)
    squares = lax.psum(jnp.sum(widened * widened, axis=1), "dp")
    inv_rms = lax.rsqrt(squares / D + 1e-05)
    normed = (widened * inv_rms[:, None] * norm_gain.astype(jnp.float32)[None, :]).astype(
        jnp.bfloat16
    )
    gate_part = jnp.dot(normed, gate_weight, preferred_element_type=jnp.float32)
    up_part = jnp.dot(normed, up_weight, preferred_element_type=jnp.float32)
    projected = lax.psum_scatter(
        jnp.concatenate((gate_part, up_part), axis=1).astype(jnp.bfloat16),
        "dp",
        scatter_dimension=0,
        tiled=True,
    ).astype(jnp.float32)
    gate_sum = projected[:, :width_units]
    up_sum = projected[:, width_units:]
    hidden = (jax.nn.silu(gate_sum) * up_sum * keep_scale).astype(jnp.bfloat16)
    partial_value = jnp.dot(
        lax.all_gather(hidden, "dp", axis=0, tiled=True),
        down_weight,
        preferred_element_type=jnp.float32,
    )
    mlp_sum = lax.psum_scatter(
        partial_value.astype(jnp.bfloat16), "tensor", scatter_dimension=0, tiled=True
    ).astype(jnp.float32)
    out_rows = mlp_sum.shape[0]
    first_row = lax.axis_index("tensor") * out_rows
    residual = lax.dynamic_slice_in_dim(collected, first_row, out_rows, 0)
    layer_out = (residual.astype(jnp.float32) + mlp_sum).astype(jnp.bfloat16)
    widened_out = layer_out.astype(jnp.float32)
    row_check = lax.psum(jnp.sum(widened_out * widened_out, axis=1), "dp") / D
    return (layer_out, row_check)


def solution(mesh):
    placed = (
        P(("dp", "tensor"), None),
        P(("dp", "tensor"), None),
        P("dp"),
        P("dp", "tensor"),
        P("dp", "tensor"),
        P("tensor", "dp"),
    )
    return jax.shard_map(
        on_device,
        mesh=mesh,
        in_specs=placed,
        out_specs=(P("tensor", "dp"), P("tensor")),
        check_vma=False,
    )
```

profile of v0, /device:TPU:0, one launch (start us, length us, event | category | flops | bytes accessed | tf_op | source)
XLA Modules:
  0.0 222.7 jit_solution(6830503011668420196)
XLA Ops:
  7.2 0.0 all-gather.3.cloned.1.call-start
  7.2 1.0 copy.31
  8.2 10.8 %all_to_all.35 = bf16[16,4,2048]{2,0,1:T(8,128)(2,1)} all-to-all(bf16[16,4,2048]{2,0,1:T(8,128)(2,1)S(1)} %bitcast.30), channel_id=1, replica_groups=mesh['dp'=4,'tensor'=8] {'dp'}, dimensions={1} | all-to-all | bytes 524288 | tf_op jit(solution)/shard_map/all_to_all | solution.py:18
  19.0 0.0 all-gather.3.cloned.1.call-update
  19.0 0.0 reduce-scatter.3.cloned.1.call-start
  19.1 0.7 convert_element_type.40
  19.8 28.3 %all-gather.3.cloned.1.call-done = bf16[512,2048]{1,0:T(8,128)(2,1)} async-done(((bf16[64,2048]{1,0:T(8,128)(2,1)}), bf16[512,2048]{1,0:T(8,128)(2,1)}) %all-gather.3.cloned.1.call-update) | async-done | bytes 2097168 | tf_op jit(solution)/shard_map/all_gather | solution.py:19
  48.1 0.0 copy-start
  48.1 1.9 copy.23
  49.9 0.3 copy-done
  50.3 0.0 copy-start.1
  50.3 0.5 multiply_reduce_fusion
  50.8 0.1 reduce_sum.21
  50.8 9.8 %psum.14 = f32[512]{0:T(512)S(1)} all-reduce(f32[512]{0:T(512)S(1)} %reduce_sum.21), channel_id=1, replica_groups=mesh['dp'=4,'tensor'=8] {'dp'}, use_global_device_ids=true, to_apply=%region_1.0 | all-reduce | flops 512 | bytes 4096 | tf_op jit(solution)/shard_map/psum | solution.py:24
  60.7 7.1 %convolution_convert_fusion.2 = bf16[512,1792]{1,0:T(8,128)(2,1)S(1)} fusion(bf16[2048,1792]{1,0:T(8,128)(2,1)} %param.9, bf16[512,2048]{1,0:T(8,128)(2,1)S(1)} %bitcast.26, f32[2048]{0:T(1024)S(1)} %convert_element_type.40, f32[512]{0:T(512)S(1)} %add_rsqrt_fusion), kind=kOutput, calls=%fused_computation.5 | convolution fusion | flops 3763208192 | bytes 11282432 | tf_op jit(solution)/shard_map/dot_general | solution.py:29
  67.8 0.0 copy-done.1
  67.8 7.1 %convolution_convert_fusion.1 = bf16[512,1792]{1,0:T(8,128)(2,1)S(1)} fusion(bf16[2048,1792]{1,0:T(8,128)(2,1)} %param.10, bf16[512,2048]{1,0:T(8,128)(2,1)S(1)} %bitcast.27, f32[2048]{0:T(1024)S(1)} %convert_element_type.40, f32[512]{0:T(512)S(1)} %add_rsqrt_fusion), kind=kOutput, calls=%fused_computation.4 | convolution fusion | flops 3763208192 | bytes 11282432 | tf_op jit(solution)/shard_map/dot_general | solution.py:30
  74.9 2.1 pad_maximum_fusion
  77.1 0.0 copy-start.2
  77.1 0.0 reduce-scatter.3.cloned.1.call-update
  77.1 0.7 copy-done.2
  77.8 0.1 all_to_all.30
  77.9 0.7 reshape.26
  78.7 3.4 %all-to-all-start.1 = ((s32[8,1,896]{2,1,0:T(1,128)}), s32[8,1,896]{2,1,0:T(1,128)S(1)}, u32[]{:S(2)}, u32[]{:S(2)}) async-start(s32[8,1,896]{2,1,0:T(1,128)} %reshape.26), calls=%async_computation.2 | async-start | bytes 57344 | tf_op jit(solution)/shard_map/all_to_all | solution.py:12
  82.0 0.0 all-gather.5.cloned.1.call-start
  82.1 0.1 shift_right_arithmetic.26
  82.2 5.5 %all-to-all-done.1 = s32[8,1,896]{2,1,0:T(1,128)S(1)} async-done(((s32[8,1,896]{2,1,0:T(1,128)}), s32[8,1,896]{2,1,0:T(1,128)S(1)}, u32[]{:S(2)}, u32[]{:S(2)}) %all-to-all-start.1) | async-done | bytes 28704 | tf_op jit(solution)/shard_map/all_to_all | solution.py:12
  87.7 0.5 broadcast.10
  88.2 0.7 reduce.1
  88.9 0.1 reshape.27
  89.0 0.1 copy.26
  89.1 0.1 shift_right_arithmetic.23
  89.1 0.3 copy.27
  89.5 33.7 %reduce-scatter.3.cloned.1.call-done = bf16[128,3584]{1,0:T(8,128)(2,1)} async-done(((bf16[512,3584]{1,0:T(8,128)(2,1)}), bf16[128,3584]{1,0:T(8,128)(2,1)}) %reduce-scatter.3.cloned.1.call-update) | async-done | bytes 917520 | tf_op jit(solution)/shard_map/reduce_scatter | solution.py:31
  123.1 1.4 convert_element_type.42
  124.5 1.1 fusion.1
  125.6 0.0 all-gather.5.cloned.1.call-update
  125.6 0.0 reduce-scatter.5.cloned.1.call-start
  125.7 33.1 %all-gather.5.cloned.1.call-done = bf16[512,1792]{1,0:T(8,128)(2,1)} async-done(((bf16[128,1792]{1,0:T(8,128)(2,1)}), bf16[512,1792]{1,0:T(8,128)(2,1)}) %all-gather.5.cloned.1.call-update) | async-done | bytes 1835024 | tf_op jit(solution)/shard_map/all_gather | solution.py:41
  158.8 8.9 %convolution_convert_fusion = bf16[512,2048]{1,0:T(8,128)(2,1)} fusion(bf16[512,1792]{1,0:T(8,128)(2,1)} %all-gather.5.cloned.1.call-done, bf16[1792,2048]{1,0:T(8,128)(2,1)} %param.11), kind=kOutput, calls=%fused_computation.3 | convolution fusion | flops 3759144960 | bytes 11272192 | tf_op jit(solution)/shard_map/dot_general | solution.py:40
  167.7 0.0 reduce-scatter.5.cloned.1.call-update
  167.7 36.2 %reduce-scatter.5.cloned.1.call-done = bf16[64,2048]{1,0:T(8,128)(2,1)} async-done(((bf16[512,2048]{1,0:T(8,128)(2,1)}), bf16[64,2048]{1,0:T(8,128)(2,1)}) %reduce-scatter.5.cloned.1.call-update) | async-done | bytes 262160 | tf_op jit(solution)/shard_map/reduce_scatter | solution.py:45
  204.0 1.9 multiply_reduce_fusion.1
  205.9 9.8 %psum.15 = f32[64]{0:T(128)S(1)} all-reduce(f32[64]{0:T(128)S(1)} %get-tuple-element.2), channel_id=1, replica_groups=mesh['dp'=4,'tensor'=8] {'dp'}, use_global_device_ids=true, to_apply=%region_5.6 | all-reduce | flops 64 | bytes 512 | tf_op jit(solution)/shard_map/psum | solution.py:53
  215.7 0.5 broadcast_multiply_fusion
  (4 shorter events, 0.0 us)
Async XLA Ops:
  7.2 40.9 %all-gather.3.cloned.1.call-start = ((), (), s32[]{:S(2)}) async-start(), calls=%async_computation.4 | async-start | bytes 2359296 | tf_op jit(solution)/shard_map/all_gather | solution.py:19
  19.0 104.1 %reduce-scatter.3.cloned.1.call-start = ((), (), s32[]{:S(2)}) async-start(), calls=%async_computation.5 | async-start | bytes 4587520 | tf_op jit(solution)/shard_map/reduce_scatter | solution.py:31
  48.1 2.2 copy-start
  50.3 17.5 %copy-start.1 = (bf16[4,8,16,2048]{3,2,1,0:T(8,128)(2,1)}, bf16[4,8,16,2048]{3,2,1,0:T(8,128)(2,1)S(1)}, u32[]{:S(2)}) copy-start(bf16[4,8,16,2048]{3,2,1,0:T(8,128)(2,1)S(1)} %copy.23) | copy-start | bytes 6291460
  77.1 0.8 copy-start.2
  78.7 9.0 %all-to-all-start.1 = ((s32[8,1,896]{2,1,0:T(1,128)}), s32[8,1,896]{2,1,0:T(1,128)S(1)}, u32[]{:S(2)}, u32[]{:S(2)}) async-start(s32[8,1,896]{2,1,0:T(1,128)} %reshape.26), calls=%async_computation.2 | async-start | bytes 57344 | tf_op jit(solution)/shard_map/all_to_all | solution.py:12
  82.0 76.8 %all-gather.5.cloned.1.call-start = ((), (), s32[]{:S(2)}) async-start(), calls=%async_computation.6 | async-start | bytes 2293760 | tf_op jit(solution)/shard_map/all_gather | solution.py:41
  125.6 78.3 %reduce-scatter.5.cloned.1.call-start = ((), (), s32[]{:S(2)}) async-start(), calls=%async_computation.7 | async-start | bytes 2359296 | tf_op jit(solution)/shard_map/reduce_scatter | solution.py:45
Sparse Core Ops, SparseCore 0:
  19.1 28.8 all-gather.2
  77.2 45.8 reduce-scatter.2
  125.7 33.0 all-gather.4
  167.8 36.0 reduce-scatter.4
where the time goes:
time: 223 us
  waiting for transfers between devices  137 us (61%)
  blocking collectives  30.4 us (14%)
  matrix products  23.1 us (10%)
  between operations  13.9 us (6%)
  other arithmetic  8.92 us (4%)
  local copies, waits for them, and re-layouts  5.94 us (3%)
  starting transfers between devices  3.51 us (2%)
    reduce_scatter x1, waiting for transfers between devices, on_device(): lax.psum_scatter(partial_value.astype(jnp.bfloat16), 'tensor', scatter_di...  36.2 us
    reduce_scatter x1, waiting for transfers between devices, on_device(): lax.psum_scatter(jnp.concatenate((gate_part, up_part), axis=1).astype(jnp...  33.7 us
    all_gather x1, waiting for transfers between devices, on_device(): lax.all_gather(hidden, 'dp', axis=0, tiled=True)  33.1 us
    all_gather x1, waiting for transfers between devices, on_device(): collected = lax.all_gather(columns, 'tensor', axis=0, tiled=True)  28.3 us
    all_to_all x1, blocking collectives, on_device(): lax.all_to_all(saved_input, 'dp', split_axis=1, concat_axis=0, tiled=True)  10.8 us
    psum x1, blocking collectives, on_device(): squares = lax.psum(jnp.sum(widened * widened, axis=1), 'dp')  9.83 us
    psum x1, blocking collectives, on_device(): row_check = lax.psum(jnp.sum(widened_out * widened_out, axis=1), 'dp') / D  9.79 us
    dot_general x1, matrix products, on_device(): jnp.dot(lax.all_gather(hidden, 'dp', axis=0, tiled=True), down_weight, pr...  8.89 us
  transfers between devices with their start and end apart: 5, of which 5 were waited for; matrix products, arithmetic and copies ran while one was open for 1% of the time, Pallas kernels for 0%

commit v1 on v0

--- a/solution.py
+++ b/solution.py
@@ -16,7 +16,9 @@
     keep_scale = 2.0 * keep_mask.astype(jnp.float32)
     width_units = gate_weight.shape[1]
     columns = lax.all_to_all(saved_input, "dp", split_axis=1, concat_axis=0, tiled=True)
-    collected = lax.all_gather(columns, "tensor", axis=0, tiled=True)
+    collected = jnp.concatenate(
+        lax.all_to_all(jnp.stack([columns] * lax.axis_size("tensor")), "tensor", 0, 0), axis=0
+    )
     per_device = saved_input.shape[0]
     collected = collected.reshape(tensor_width, dp_width, per_device, collected.shape[1])
     collected = collected.transpose(1, 0, 2, 3).reshape(-1, collected.shape[3])

time: 223 us -> 249 us (1.12)
  waiting for transfers between devices: 137 us -> 158 us
  starting transfers between devices: 3.51 us -> 8.34 us
    all_to_all x0 -> x1, waiting for transfers between devices: none -> 49 us  [on_device(): lax.all_to_all(jnp.stack([columns] * lax.axis_size('tensor')), 'tensor',...]
    all_gather x1 -> x0, waiting for transfers between devices: 28.3 us -> none  [on_device(): collected = lax.all_gather(columns, 'tensor', axis=0, tiled=True)]
    all_to_all x0 -> x1, starting transfers between devices: none -> 4.88 us  [on_device(): lax.all_to_all(jnp.stack([columns] * lax.axis_size('tensor')), 'tensor',...]
where the time goes in v1:
time: 249 us; the launch traced here: 248 us
  waiting for transfers between devices  158 us (63%)
  blocking collectives  28.9 us (12%)
  matrix products  23.9 us (10%)
  between operations  13.9 us (6%)
  starting transfers between devices  8.34 us (3%)
  other arithmetic  8.24 us (3%)
  local copies, waits for them, and re-layouts  6.83 us (3%)
    all_to_all x1, waiting for transfers between devices, on_device(): lax.all_to_all(jnp.stack([columns] * lax.axis_size('tensor')), 'tensor',...  49 us
    reduce_scatter x1, waiting for transfers between devices, on_device(): lax.psum_scatter(partial_value.astype(jnp.bfloat16), 'tensor', scatter_di...  36.2 us
    reduce_scatter x1, waiting for transfers between devices, on_device(): lax.psum_scatter(jnp.concatenate((gate_part, up_part), axis=1).astype(jnp...  34 us
    all_gather x1, waiting for transfers between devices, on_device(): lax.all_gather(hidden, 'dp', axis=0, tiled=True)  33.1 us
    all_to_all x1, blocking collectives, on_device(): lax.all_to_all(saved_input, 'dp', split_axis=1, concat_axis=0, tiled=True)  10.7 us
    psum x1, blocking collectives, on_device(): row_check = lax.psum(jnp.sum(widened_out * widened_out, axis=1), 'dp') / D  9.79 us
    dot_general x1, matrix products, on_device(): jnp.dot(lax.all_gather(hidden, 'dp', axis=0, tiled=True), down_weight, pr...  8.89 us
    psum x1, blocking collectives, on_device(): squares = lax.psum(jnp.sum(widened * widened, axis=1), 'dp')  8.37 us
  transfers between devices with their start and end apart: 5, of which 5 were waited for; matrix products, arithmetic and copies ran while one was open for 1% of the time, Pallas kernels for 0%

profile of v1, /device:TPU:0, one launch (start us, length us, event | category | flops | bytes accessed | tf_op | source)
XLA Modules:
  0.0 247.9 jit_solution(18390814775954757363)
XLA Ops:
  7.2 1.0 copy.31
  8.1 0.0 copy-start.2
  8.1 10.7 %all_to_all.37 = bf16[16,4,2048]{2,0,1:T(8,128)(2,1)S(1)} all-to-all(bf16[16,4,2048]{2,0,1:T(8,128)(2,1)S(1)} %bitcast.30), channel_id=1, replica_groups=mesh['dp'=4,'tensor'=8] {'dp'}, dimensions={1} | all-to-all | bytes 524288 | tf_op jit(solution)/shard_map/all_to_all | solution.py:18
  18.9 1.6 stack.5
  20.5 4.9 %all-to-all-start.1 = ((bf16[8,64,2048]{2,1,0:T(8,128)(2,1)}), bf16[8,64,2048]{2,1,0:T(8,128)(2,1)S(1)}, u32[]{:S(2)}, u32[]{:S(2)}) async-start(bf16[8,64,2048]{2,1,0:T(8,128)(2,1)} %stack.5), calls=%async_computation.1 | async-start | bytes 4194304 | tf_op jit(solution)/shard_map/all_to_all | solution.py:20
  25.4 0.0 reduce-scatter.3.cloned.1.call-start
  25.4 0.0 copy-done.2
  25.4 49.0 %all-to-all-done.1 = bf16[8,64,2048]{2,1,0:T(8,128)(2,1)S(1)} async-done(((bf16[8,64,2048]{2,1,0:T(8,128)(2,1)}), bf16[8,64,2048]{2,1,0:T(8,128)(2,1)S(1)}, u32[]{:S(2)}, u32[]{:S(2)}) %all-to-all-start.1) | async-done | bytes 2097184 | tf_op jit(solution)/shard_map/all_to_all | solution.py:20
  74.4 1.5 copy.23
  75.9 0.5 multiply_reduce_fusion
  76.4 0.1 reduce_sum.21
  76.4 8.4 %psum.14 = f32[512]{0:T(512)S(1)} all-reduce(f32[512]{0:T(512)S(1)} %reduce_sum.21), channel_id=1, replica_groups=mesh['dp'=4,'tensor'=8] {'dp'}, use_global_device_ids=true, to_apply=%region_1.0 | all-reduce | flops 512 | bytes 4096 | tf_op jit(solution)/shard_map/psum | solution.py:26
  84.8 0.0 copy-start
  84.8 7.9 %convolution_convert_fusion.2 = bf16[512,1792]{1,0:T(8,128)(2,1)S(1)} fusion(bf16[2048,1792]{1,0:T(8,128)(2,1)} %param.9, bf16[512,2048]{1,0:T(8,128)(2,1)} %bitcast.26, f32[2048]{0:T(1024)S(1)} %convert_element_type.40, f32[512]{0:T(512)S(1)} %add_rsqrt_fusion), kind=kOutput, calls=%fused_computation.5 | convolution fusion | flops 3763208192 | bytes 11282432 | tf_op jit(solution)/shard_map/dot_general | solution.py:31
  92.7 0.0 copy-done
  92.7 7.1 %convolution_convert_fusion.1 = bf16[512,1792]{1,0:T(8,128)(2,1)S(1)} fusion(bf16[2048,1792]{1,0:T(8,128)(2,1)} %param.10, bf16[512,2048]{1,0:T(8,128)(2,1)S(1)} %bitcast.28, f32[2048]{0:T(1024)S(1)} %convert_element_type.40, f32[512]{0:T(512)S(1)} %add_rsqrt_fusion), kind=kOutput, calls=%fused_computation.4 | convolution fusion | flops 3763208192 | bytes 11282432 | tf_op jit(solution)/shard_map/dot_general | solution.py:32
  99.8 2.1 pad_maximum_fusion
  101.9 0.0 copy-start.1
  101.9 0.0 reduce-scatter.3.cloned.1.call-update
  102.0 0.7 copy-done.1
  102.7 0.1 all_to_all.31
  102.8 0.7 reshape.25
  103.5 3.3 %all-to-all-start.2 = ((s32[8,1,896]{2,1,0:T(1,128)}), s32[8,1,896]{2,1,0:T(1,128)S(1)}, u32[]{:S(2)}, u32[]{:S(2)}) async-start(s32[8,1,896]{2,1,0:T(1,128)} %reshape.25), calls=%async_computation.3 | async-start | bytes 57344 | tf_op jit(solution)/shard_map/all_to_all | solution.py:12
  106.9 0.0 all-gather.2.cloned.1.call-start
  107.0 0.1 shift_right_arithmetic.26
  107.0 5.5 %all-to-all-done.2 = s32[8,1,896]{2,1,0:T(1,128)S(1)} async-done(((s32[8,1,896]{2,1,0:T(1,128)}), s32[8,1,896]{2,1,0:T(1,128)S(1)}, u32[]{:S(2)}, u32[]{:S(2)}) %all-to-all-start.2) | async-done | bytes 28704 | tf_op jit(solution)/shard_map/all_to_all | solution.py:12
  112.5 0.5 broadcast.11
  113.1 0.7 reduce.1
  113.8 0.1 reshape.26
  113.9 0.1 copy.26
  113.9 0.1 shift_right_arithmetic.23
  114.0 0.3 copy.27
  114.3 34.0 %reduce-scatter.3.cloned.1.call-done = bf16[128,3584]{1,0:T(8,128)(2,1)} async-done(((bf16[512,3584]{1,0:T(8,128)(2,1)}), bf16[128,3584]{1,0:T(8,128)(2,1)}) %reduce-scatter.3.cloned.1.call-update) | async-done | bytes 917520 | tf_op jit(solution)/shard_map/reduce_scatter | solution.py:33
  148.3 1.4 convert_element_type.42
  149.7 1.1 fusion.1
  150.8 0.0 all-gather.2.cloned.1.call-update
  150.8 0.0 reduce-scatter.5.cloned.1.call-start
  150.9 33.1 %all-gather.2.cloned.1.call-done = bf16[512,1792]{1,0:T(8,128)(2,1)} async-done(((bf16[128,1792]{1,0:T(8,128)(2,1)}), bf16[512,1792]{1,0:T(8,128)(2,1)}) %all-gather.2.cloned.1.call-update) | async-done | bytes 1835024 | tf_op jit(solution)/shard_map/all_gather | solution.py:43
  184.0 8.9 %convolution_convert_fusion = bf16[512,2048]{1,0:T(8,128)(2,1)} fusion(bf16[512,1792]{1,0:T(8,128)(2,1)} %all-gather.2.cloned.1.call-done, bf16[1792,2048]{1,0:T(8,128)(2,1)} %param.11), kind=kOutput, calls=%fused_computation.3 | convolution fusion | flops 3759144960 | bytes 11272192 | tf_op jit(solution)/shard_map/dot_general | solution.py:42
  192.9 0.0 reduce-scatter.5.cloned.1.call-update
  192.9 36.2 %reduce-scatter.5.cloned.1.call-done = bf16[64,2048]{1,0:T(8,128)(2,1)} async-done(((bf16[512,2048]{1,0:T(8,128)(2,1)}), bf16[64,2048]{1,0:T(8,128)(2,1)}) %reduce-scatter.5.cloned.1.call-update) | async-done | bytes 262160 | tf_op jit(solution)/shard_map/reduce_scatter | solution.py:47
  229.2 1.9 multiply_reduce_fusion.1
  231.1 9.8 %psum.15 = f32[64]{0:T(128)S(1)} all-reduce(f32[64]{0:T(128)S(1)} %get-tuple-element.2), channel_id=1, replica_groups=mesh['dp'=4,'tensor'=8] {'dp'}, use_global_device_ids=true, to_apply=%region_5.6 | all-reduce | flops 64 | bytes 512 | tf_op jit(solution)/shard_map/psum | solution.py:55
  240.9 0.5 broadcast_multiply_fusion
  (5 shorter events, 0.0 us)
Async XLA Ops:
  8.1 17.3 %copy-start.2 = (bf16[2048]{0:T(1024)(128)(2,1)S(1)}, bf16[2048]{0:T(1024)(128)(2,1)}, u32[]{:S(2)}) copy-start(bf16[2048]{0:T(1024)(128)(2,1)} %param.8) | copy-start | bytes 12292
  20.5 53.9 %all-to-all-start.1 = ((bf16[8,64,2048]{2,1,0:T(8,128)(2,1)}), bf16[8,64,2048]{2,1,0:T(8,128)(2,1)S(1)}, u32[]{:S(2)}, u32[]{:S(2)}) async-start(bf16[8,64,2048]{2,1,0:T(8,128)(2,1)} %stack.5), calls=%async_computation.1 | async-start | bytes 4194304 | tf_op jit(solution)/shard_map/all_to_all | solution.py:20
  25.4 123.0 %reduce-scatter.3.cloned.1.call-start = ((), (), s32[]{:S(2)}) async-start(), calls=%async_computation.5 | async-start | bytes 4587520 | tf_op jit(solution)/shard_map/reduce_scatter | solution.py:33
  84.8 7.9 %copy-start = (bf16[4,8,16,2048]{3,2,1,0:T(8,128)(2,1)S(1)}, bf16[4,8,16,2048]{3,2,1,0:T(8,128)(2,1)}, u32[]{:S(2)}) copy-start(bf16[4,8,16,2048]{3,2,1,0:T(8,128)(2,1)} %copy.23) | copy-start | bytes 6291460
  101.9 0.8 copy-start.1
  103.5 9.0 %all-to-all-start.2 = ((s32[8,1,896]{2,1,0:T(1,128)}), s32[8,1,896]{2,1,0:T(1,128)S(1)}, u32[]{:S(2)}, u32[]{:S(2)}) async-start(s32[8,1,896]{2,1,0:T(1,128)} %reshape.25), calls=%async_computation.3 | async-start | bytes 57344 | tf_op jit(solution)/shard_map/all_to_all | solution.py:12
  106.9 77.1 %all-gather.2.cloned.1.call-start = ((), (), s32[]{:S(2)}) async-start(), calls=%async_computation.6 | async-start | bytes 2293760 | tf_op jit(solution)/shard_map/all_gather | solution.py:43
  150.8 78.3 %reduce-scatter.5.cloned.1.call-start = ((), (), s32[]{:S(2)}) async-start(), calls=%async_computation.7 | async-start | bytes 2359296 | tf_op jit(solution)/shard_map/reduce_scatter | solution.py:47
Sparse Core Ops, SparseCore 0:
  102.1 46.1 reduce-scatter.2
  151.0 33.0 all-gather.1
  193.1 36.0 reduce-scatter.4
